TPU v7x, 128 devices: a whole 4x4x4 slice. The times are simulated.
128 devices in a mesh: sec: 64 (over x, y, z), node: 2 (over core).
Axes of the slice: x: 4, y: 4, z: 4, core: 2. Of those that a mesh axis runs over, the one named last changes fastest.
Arguments:
- env_blocks: bfloat16 [2, 24576, 128, 128], P('node', 'sec'), may hold values from -10 to 10, as said below
- iso_blocks: bfloat16 [2, 24576, 128, 128], P('node', 'sec'), may hold values from -6 to 6
- joined_sector: int32 [2, 24576], P('node', 'sec'), may hold values from 0 to 63, as said below
- owner_map: int32 [2, 64], P('node'), may hold values from 0 to 63, each once within a row
- live_pairs: int32 [2, 64], P('node', 'sec'), may hold values from 1 to 384, as said below
Outputs:
- environment: float32 [2, 64, 128, 128], P('node', 'sec')
Inputs may be any that keep to these rules, and one draw needn't show every extreme that they name: `env_blocks`: each block is symmetric. `joined_sector`: slot p belongs to tree node k = p // 3072 of its group, and its sector is one of that node's sectors k * 8 to k * 8 + 7. `owner_map`: each row names every index once. `live_pairs`: in every group some index of sec has all 384 slots live.
All inputs are finite; a program needn't handle non-finite values.
Results may differ from a plain program's by a relative error of at most 0.0003.
Values sent between devices are 32-bit elements; how exact they have to be, the bound alone decides.
No kernel may reach another device: no remote copies, remote signals or barrier semaphores. Data moves between devices by JAX's collectives and lax.ppermute only.
A program may use at most 128 MiB of HBM per device.

v0:
```python
import jax
import jax.numpy as jnp
from jax import lax
from jax.sharding import Mesh
from jax.sharding import PartitionSpec as P

SEC = ("sec_0", "sec_1", "sec_2")
SEC_NODE = ("sec_0", "sec_1", "sec_2", "node")


pair_group = 32


def cut_along(shard, dim, length):
    shape = shard.shape
    blocks = shard.reshape(*shape[:dim], length, shape[dim] // length, *shape[dim + 1 :])
    return jnp.moveaxis(blocks, dim, 0)


def sum_at_owner(shard, axis, dim):
    length = lax.axis_size(axis)
    blocks = lax.all_to_all(cut_along(shard, dim, length), axis, 0, 0, tiled=True)
    return jnp.sum(blocks, axis=0)


def by_axis(shard, axes):
    for axis in axes:
        shard = lax.psum(shard, axis)
    return shard


def body(env_blocks, iso_blocks, joined_sector, owner_map, live_pairs):
    pairs_here = env_blocks.shape[1]
    sector_width = iso_blocks.shape[3]
    half_width = sector_width // 2
    sectors = lax.axis_size(SEC)
    sector_ids = jnp.arange(sectors, dtype=jnp.int32)
    matches = joined_sector[0][:, None] == sector_ids[None, :]
    targets = jnp.sum(jnp.where(matches, owner_map[0][None, :], 0), axis=1)
    living = jnp.arange(pairs_here, dtype=jnp.int32) < live_pairs[0, 0]

    def add_group(turn_index, partial_value):
        first_pair = turn_index * pair_group
        blocks = lax.dynamic_slice_in_dim(env_blocks[0], first_pair, pair_group, 0)
        weights = lax.dynamic_slice_in_dim(iso_blocks[0], first_pair, pair_group, 0)
        group_targets = lax.dynamic_slice_in_dim(targets, first_pair, pair_group, 0)
        group_live = lax.dynamic_slice_in_dim(living, first_pair, pair_group, 0)
        product = jnp.einsum(
            "prk,pkc->prc", blocks, weights, preferred_element_type=jnp.float32
        ).astype(jnp.bfloat16)
        sandwich = jnp.einsum("prc,prd->pcd", weights, product, preferred_element_type=jnp.float32)
        selector = ((group_targets[:, None] == sector_ids[None, :]) & group_live[:, None]).astype(
            jnp.float32
        )
        flat_terms = sandwich.reshape(pair_group, sector_width * sector_width)
        added = lax.dot_general(
            selector,
            flat_terms,
            (((0,), (0,)), ((), ())),
            precision=lax.Precision.HIGHEST,
            preferred_element_type=jnp.float32,
        )
        return partial_value + added

    zero_sums = jnp.zeros((sectors, sector_width * sector_width), jnp.float32)
    turn_total = pairs_here // pair_group
    partial_value = lax.fori_loop(0, turn_total, add_group, zero_sums).reshape(
        sectors, sector_width, sector_width
    )
    upper_left = partial_value[:, :half_width, :half_width]
    upper_right = partial_value[:, :half_width, half_width:]
    lower_right = partial_value[:, half_width:, half_width:]
    corners = jnp.triu(upper_left) + jnp.tril(jnp.swapaxes(lower_right, 1, 2), -1)
    diagonal_row = jnp.diagonal(lower_right, axis1=1, axis2=2)[:, None, :]
    packed = jnp.concatenate((corners, upper_right, diagonal_row), axis=1)
    summed = sum_at_owner(packed, SEC, 0)[0]
    corners_sum = summed[:half_width]
    right_sum = summed[half_width : 2 * half_width]
    diagonal_sum = summed[2 * half_width]
    left_block = jnp.triu(corners_sum) + jnp.triu(corners_sum, 1).T
    lower_upper = jnp.tril(corners_sum, -1).T + jnp.diag(diagonal_sum)
    right_block = lower_upper + jnp.triu(lower_upper, 1).T
    top_rows = jnp.concatenate((left_block, right_sum), axis=1)
    bottom_rows = jnp.concatenate((right_sum.T, right_block), axis=1)
    hermitian = jnp.concatenate((top_rows, bottom_rows), axis=0)
    squares = jnp.sum(hermitian * hermitian)
    grand_total = by_axis(squares, SEC_NODE)
    entries = sectors * lax.axis_size("node") * sector_width * sector_width
    factor = lax.rsqrt(grand_total / entries + 1e-06)
    return (hermitian * factor)[None, None]


def solution(mesh):
    split = Mesh(
        mesh.devices.reshape(4, 4, 4, mesh.shape["node"]), ("sec_0", "sec_1", "sec_2", "node")
    )
    placed = (
        P("node", SEC, None, None),
        P("node", SEC, None, None),
        P("node", SEC),
        P("node", None),
        P("node", SEC),
    )
    return jax.shard_map(
        body, mesh=split, in_specs=placed, out_specs=P("node", SEC, None, None), check_vma=False
    )
```

profile of v0, /device:TPU:1, one launch (start us, length us, event | category | flops | bytes accessed | tf_op | source)
XLA Modules:
  0.0 255.1 jit_solution(2081290549324022647)
XLA Ops:
  0.0 0.7 reduce.1
  1.4 0.7 select_reduce_fusion
  2.1 121.4 %while.14 = (s32[]{:T(128)}, f32[64,16384]{1,0:T(8,128)}, s32[384]{0:T(512)S(1)}, pred[384]{0:T(512)(128)(4,1)S(1)}, bf16[1,384,128,128]{3,2,1,0:T(8,128)(2,1)},...) while((s32[]{:T(128)}, f32[64,16384]{1,0:T(8,128)}, ...), condition=%wide.region_2.3_spmd.clone, body=%wide.region_1.2_spmd.clone.sunk | while | flops 673714176 | bytes 15730821 | solution.py:67
  2.1 2.6 %fusion.36 = f32[32,128,128]{2,1,0:T(8,128)S(1)} fusion(bf16[1,384,128,128]{3,2,1,0:T(8,128)(2,1)} %get-tuple-element.248, s32[]{:T(128)S(6)} %select_n.72, bf16[1,384,128,128]{3,2,1,0:T(8,128)(2,1)} %get-tuple-element.247), kind=kOutput, calls=%fused_computation.6.clone.1 | convolution fusion | flops 268959744 | bytes 5244416 | tf_op jit(solution)/shard_map/while/body/eval_jaxpr/prc,prd->pcd/dot_general | solution.py:51
  4.8 0.1 dynamic_slice.54
  4.8 0.1 dynamic_slice.55
  4.9 5.3 %convolution_add_fusion.2 = f32[64,16384]{1,0:T(8,128)} fusion(f32[64,16384]{1,0:T(8,128)} %get-tuple-element.234, f32[4,8,128,128]{3,2,1,0:T(8,128)S(1)} %bitcast.64, pred[]{:T(512)S(6)} %compare.3, s32[32]{0:T(128)S(1)} %dynamic_slice.54, pred[32]{0:T(512)(128)(4,1)S(1)} %dynamic_slice.55), kind=kOutput, calls=%fused_computation.2.clone.1 | convolution fusion | flops 404754432 | bytes 10485921 | tf_op jit(solution)/shard_map/while/body/eval_jaxpr/dot_general | solution.py:56
  10.2 2.6 %fusion.36 = f32[32,128,128]{2,1,0:T(8,128)S(1)} fusion(bf16[1,384,128,128]{3,2,1,0:T(8,128)(2,1)} %get-tuple-element.248, s32[]{:T(128)S(6)} %select_n.72, bf16[1,384,128,128]{3,2,1,0:T(8,128)(2,1)} %get-tuple-element.247), kind=kOutput, calls=%fused_computation.6.clone.1 | convolution fusion | flops 268959744 | bytes 5244416 | tf_op jit(solution)/shard_map/while/body/eval_jaxpr/prc,prd->pcd/dot_general | solution.py:51
  12.8 0.1 dynamic_slice.54
  13.0 7.5 %convolution_add_fusion.2 = f32[64,16384]{1,0:T(8,128)} fusion(f32[64,16384]{1,0:T(8,128)} %get-tuple-element.234, f32[4,8,128,128]{3,2,1,0:T(8,128)S(1)} %bitcast.64, pred[]{:T(512)S(6)} %compare.3, s32[32]{0:T(128)S(1)} %dynamic_slice.54, pred[32]{0:T(512)(128)(4,1)S(1)} %dynamic_slice.55), kind=kOutput, calls=%fused_computation.2.clone.1 | convolution fusion | flops 404754432 | bytes 10485921 | tf_op jit(solution)/shard_map/while/body/eval_jaxpr/dot_general | solution.py:56
  20.5 2.6 %fusion.36 = f32[32,128,128]{2,1,0:T(8,128)S(1)} fusion(bf16[1,384,128,128]{3,2,1,0:T(8,128)(2,1)} %get-tuple-element.248, s32[]{:T(128)S(6)} %select_n.72, bf16[1,384,128,128]{3,2,1,0:T(8,128)(2,1)} %get-tuple-element.247), kind=kOutput, calls=%fused_computation.6.clone.1 | convolution fusion | flops 268959744 | bytes 5244416 | tf_op jit(solution)/shard_map/while/body/eval_jaxpr/prc,prd->pcd/dot_general | solution.py:51
  23.1 0.1 dynamic_slice.54
  23.3 7.5 %convolution_add_fusion.2 = f32[64,16384]{1,0:T(8,128)} fusion(f32[64,16384]{1,0:T(8,128)} %get-tuple-element.234, f32[4,8,128,128]{3,2,1,0:T(8,128)S(1)} %bitcast.64, pred[]{:T(512)S(6)} %compare.3, s32[32]{0:T(128)S(1)} %dynamic_slice.54, pred[32]{0:T(512)(128)(4,1)S(1)} %dynamic_slice.55), kind=kOutput, calls=%fused_computation.2.clone.1 | convolution fusion | flops 404754432 | bytes 10485921 | tf_op jit(solution)/shard_map/while/body/eval_jaxpr/dot_general | solution.py:56
  30.8 2.6 %fusion.36 = f32[32,128,128]{2,1,0:T(8,128)S(1)} fusion(bf16[1,384,128,128]{3,2,1,0:T(8,128)(2,1)} %get-tuple-element.248, s32[]{:T(128)S(6)} %select_n.72, bf16[1,384,128,128]{3,2,1,0:T(8,128)(2,1)} %get-tuple-element.247), kind=kOutput, calls=%fused_computation.6.clone.1 | convolution fusion | flops 268959744 | bytes 5244416 | tf_op jit(solution)/shard_map/while/body/eval_jaxpr/prc,prd->pcd/dot_general | solution.py:51
  33.4 0.1 dynamic_slice.54
  33.5 0.1 dynamic_slice.55
  33.5 7.5 %convolution_add_fusion.2 = f32[64,16384]{1,0:T(8,128)} fusion(f32[64,16384]{1,0:T(8,128)} %get-tuple-element.234, f32[4,8,128,128]{3,2,1,0:T(8,128)S(1)} %bitcast.64, pred[]{:T(512)S(6)} %compare.3, s32[32]{0:T(128)S(1)} %dynamic_slice.54, pred[32]{0:T(512)(128)(4,1)S(1)} %dynamic_slice.55), kind=kOutput, calls=%fused_computation.2.clone.1 | convolution fusion | flops 404754432 | bytes 10485921 | tf_op jit(solution)/shard_map/while/body/eval_jaxpr/dot_general | solution.py:56
  41.0 2.6 %fusion.36 = f32[32,128,128]{2,1,0:T(8,128)S(1)} fusion(bf16[1,384,128,128]{3,2,1,0:T(8,128)(2,1)} %get-tuple-element.248, s32[]{:T(128)S(6)} %select_n.72, bf16[1,384,128,128]{3,2,1,0:T(8,128)(2,1)} %get-tuple-element.247), kind=kOutput, calls=%fused_computation.6.clone.1 | convolution fusion | flops 268959744 | bytes 5244416 | tf_op jit(solution)/shard_map/while/body/eval_jaxpr/prc,prd->pcd/dot_general | solution.py:51
  43.7 0.1 dynamic_slice.54
  43.8 7.5 %convolution_add_fusion.2 = f32[64,16384]{1,0:T(8,128)} fusion(f32[64,16384]{1,0:T(8,128)} %get-tuple-element.234, f32[4,8,128,128]{3,2,1,0:T(8,128)S(1)} %bitcast.64, pred[]{:T(512)S(6)} %compare.3, s32[32]{0:T(128)S(1)} %dynamic_slice.54, pred[32]{0:T(512)(128)(4,1)S(1)} %dynamic_slice.55), kind=kOutput, calls=%fused_computation.2.clone.1 | convolution fusion | flops 404754432 | bytes 10485921 | tf_op jit(solution)/shard_map/while/body/eval_jaxpr/dot_general | solution.py:56
  51.3 2.6 %fusion.36 = f32[32,128,128]{2,1,0:T(8,128)S(1)} fusion(bf16[1,384,128,128]{3,2,1,0:T(8,128)(2,1)} %get-tuple-element.248, s32[]{:T(128)S(6)} %select_n.72, bf16[1,384,128,128]{3,2,1,0:T(8,128)(2,1)} %get-tuple-element.247), kind=kOutput, calls=%fused_computation.6.clone.1 | convolution fusion | flops 268959744 | bytes 5244416 | tf_op jit(solution)/shard_map/while/body/eval_jaxpr/prc,prd->pcd/dot_general | solution.py:51
  54.0 0.1 dynamic_slice.54
  54.1 7.5 %convolution_add_fusion.2 = f32[64,16384]{1,0:T(8,128)} fusion(f32[64,16384]{1,0:T(8,128)} %get-tuple-element.234, f32[4,8,128,128]{3,2,1,0:T(8,128)S(1)} %bitcast.64, pred[]{:T(512)S(6)} %compare.3, s32[32]{0:T(128)S(1)} %dynamic_slice.54, pred[32]{0:T(512)(128)(4,1)S(1)} %dynamic_slice.55), kind=kOutput, calls=%fused_computation.2.clone.1 | convolution fusion | flops 404754432 | bytes 10485921 | tf_op jit(solution)/shard_map/while/body/eval_jaxpr/dot_general | solution.py:56
  61.6 2.8 %fusion.36 = f32[32,128,128]{2,1,0:T(8,128)S(1)} fusion(bf16[1,384,128,128]{3,2,1,0:T(8,128)(2,1)} %get-tuple-element.248, s32[]{:T(128)S(6)} %select_n.72, bf16[1,384,128,128]{3,2,1,0:T(8,128)(2,1)} %get-tuple-element.247), kind=kOutput, calls=%fused_computation.6.clone.1 | convolution fusion | flops 268959744 | bytes 5244416 | tf_op jit(solution)/shard_map/while/body/eval_jaxpr/prc,prd->pcd/dot_general | solution.py:51
  64.4 0.1 dynamic_slice.54
  64.6 7.5 %convolution_add_fusion.2 = f32[64,16384]{1,0:T(8,128)} fusion(f32[64,16384]{1,0:T(8,128)} %get-tuple-element.234, f32[4,8,128,128]{3,2,1,0:T(8,128)S(1)} %bitcast.64, pred[]{:T(512)S(6)} %compare.3, s32[32]{0:T(128)S(1)} %dynamic_slice.54, pred[32]{0:T(512)(128)(4,1)S(1)} %dynamic_slice.55), kind=kOutput, calls=%fused_computation.2.clone.1 | convolution fusion | flops 404754432 | bytes 10485921 | tf_op jit(solution)/shard_map/while/body/eval_jaxpr/dot_general | solution.py:56
  72.1 2.6 %fusion.36 = f32[32,128,128]{2,1,0:T(8,128)S(1)} fusion(bf16[1,384,128,128]{3,2,1,0:T(8,128)(2,1)} %get-tuple-element.248, s32[]{:T(128)S(6)} %select_n.72, bf16[1,384,128,128]{3,2,1,0:T(8,128)(2,1)} %get-tuple-element.247), kind=kOutput, calls=%fused_computation.6.clone.1 | convolution fusion | flops 268959744 | bytes 5244416 | tf_op jit(solution)/shard_map/while/body/eval_jaxpr/prc,prd->pcd/dot_general | solution.py:51
  74.7 0.1 dynamic_slice.54
  74.9 7.5 %convolution_add_fusion.2 = f32[64,16384]{1,0:T(8,128)} fusion(f32[64,16384]{1,0:T(8,128)} %get-tuple-element.234, f32[4,8,128,128]{3,2,1,0:T(8,128)S(1)} %bitcast.64, pred[]{:T(512)S(6)} %compare.3, s32[32]{0:T(128)S(1)} %dynamic_slice.54, pred[32]{0:T(512)(128)(4,1)S(1)} %dynamic_slice.55), kind=kOutput, calls=%fused_computation.2.clone.1 | convolution fusion | flops 404754432 | bytes 10485921 | tf_op jit(solution)/shard_map/while/body/eval_jaxpr/dot_general | solution.py:56
  82.4 2.6 %fusion.36 = f32[32,128,128]{2,1,0:T(8,128)S(1)} fusion(bf16[1,384,128,128]{3,2,1,0:T(8,128)(2,1)} %get-tuple-element.248, s32[]{:T(128)S(6)} %select_n.72, bf16[1,384,128,128]{3,2,1,0:T(8,128)(2,1)} %get-tuple-element.247), kind=kOutput, calls=%fused_computation.6.clone.1 | convolution fusion | flops 268959744 | bytes 5244416 | tf_op jit(solution)/shard_map/while/body/eval_jaxpr/prc,prd->pcd/dot_general | solution.py:51
  85.0 0.1 dynamic_slice.54
  85.2 7.5 %convolution_add_fusion.2 = f32[64,16384]{1,0:T(8,128)} fusion(f32[64,16384]{1,0:T(8,128)} %get-tuple-element.234, f32[4,8,128,128]{3,2,1,0:T(8,128)S(1)} %bitcast.64, pred[]{:T(512)S(6)} %compare.3, s32[32]{0:T(128)S(1)} %dynamic_slice.54, pred[32]{0:T(512)(128)(4,1)S(1)} %dynamic_slice.55), kind=kOutput, calls=%fused_computation.2.clone.1 | convolution fusion | flops 404754432 | bytes 10485921 | tf_op jit(solution)/shard_map/while/body/eval_jaxpr/dot_general | solution.py:56
  92.7 2.6 %fusion.36 = f32[32,128,128]{2,1,0:T(8,128)S(1)} fusion(bf16[1,384,128,128]{3,2,1,0:T(8,128)(2,1)} %get-tuple-element.248, s32[]{:T(128)S(6)} %select_n.72, bf16[1,384,128,128]{3,2,1,0:T(8,128)(2,1)} %get-tuple-element.247), kind=kOutput, calls=%fused_computation.6.clone.1 | convolution fusion | flops 268959744 | bytes 5244416 | tf_op jit(solution)/shard_map/while/body/eval_jaxpr/prc,prd->pcd/dot_general | solution.py:51
  95.3 0.1 dynamic_slice.54
  95.4 7.5 %convolution_add_fusion.2 = f32[64,16384]{1,0:T(8,128)} fusion(f32[64,16384]{1,0:T(8,128)} %get-tuple-element.234, f32[4,8,128,128]{3,2,1,0:T(8,128)S(1)} %bitcast.64, pred[]{:T(512)S(6)} %compare.3, s32[32]{0:T(128)S(1)} %dynamic_slice.54, pred[32]{0:T(512)(128)(4,1)S(1)} %dynamic_slice.55), kind=kOutput, calls=%fused_computation.2.clone.1 | convolution fusion | flops 404754432 | bytes 10485921 | tf_op jit(solution)/shard_map/while/body/eval_jaxpr/dot_general | solution.py:56
  102.9 2.7 %fusion.36 = f32[32,128,128]{2,1,0:T(8,128)S(1)} fusion(bf16[1,384,128,128]{3,2,1,0:T(8,128)(2,1)} %get-tuple-element.248, s32[]{:T(128)S(6)} %select_n.72, bf16[1,384,128,128]{3,2,1,0:T(8,128)(2,1)} %get-tuple-element.247), kind=kOutput, calls=%fused_computation.6.clone.1 | convolution fusion | flops 268959744 | bytes 5244416 | tf_op jit(solution)/shard_map/while/body/eval_jaxpr/prc,prd->pcd/dot_general | solution.py:51
  105.6 0.1 dynamic_slice.54
  105.8 7.5 %convolution_add_fusion.2 = f32[64,16384]{1,0:T(8,128)} fusion(f32[64,16384]{1,0:T(8,128)} %get-tuple-element.234, f32[4,8,128,128]{3,2,1,0:T(8,128)S(1)} %bitcast.64, pred[]{:T(512)S(6)} %compare.3, s32[32]{0:T(128)S(1)} %dynamic_slice.54, pred[32]{0:T(512)(128)(4,1)S(1)} %dynamic_slice.55), kind=kOutput, calls=%fused_computation.2.clone.1 | convolution fusion | flops 404754432 | bytes 10485921 | tf_op jit(solution)/shard_map/while/body/eval_jaxpr/dot_general | solution.py:56
  113.3 2.6 %fusion.36 = f32[32,128,128]{2,1,0:T(8,128)S(1)} fusion(bf16[1,384,128,128]{3,2,1,0:T(8,128)(2,1)} %get-tuple-element.248, s32[]{:T(128)S(6)} %select_n.72, bf16[1,384,128,128]{3,2,1,0:T(8,128)(2,1)} %get-tuple-element.247), kind=kOutput, calls=%fused_computation.6.clone.1 | convolution fusion | flops 268959744 | bytes 5244416 | tf_op jit(solution)/shard_map/while/body/eval_jaxpr/prc,prd->pcd/dot_general | solution.py:51
  115.9 0.1 dynamic_slice.54
  116.1 7.5 %convolution_add_fusion.2 = f32[64,16384]{1,0:T(8,128)} fusion(f32[64,16384]{1,0:T(8,128)} %get-tuple-element.234, f32[4,8,128,128]{3,2,1,0:T(8,128)S(1)} %bitcast.64, pred[]{:T(512)S(6)} %compare.3, s32[32]{0:T(128)S(1)} %dynamic_slice.54, pred[32]{0:T(512)(128)(4,1)S(1)} %dynamic_slice.55), kind=kOutput, calls=%fused_computation.2.clone.1 | convolution fusion | flops 404754432 | bytes 10485921 | tf_op jit(solution)/shard_map/while/body/eval_jaxpr/dot_general | solution.py:56
  123.6 2.9 %copy.65 = f32[8,8,128,128]{3,2,1,0:T(8,128)S(1)} copy(f32[8,8,128,128]{3,1,2,0:T(8,128)} %bitcast.65) | data formatting | bytes 8388608
  126.5 3.8 %fusion.24 = (f32[64,64,64]{2,1,0:T(8,128)}, f32[64,64,64]{2,1,0:T(8,128)}, f32[64,64,64]{2,1,0:T(8,128)}) fusion(f32[64,128,128]{2,1,0:T(8,128)S(1)} %bitcast.66), kind=kLoop, calls=%fused_computation.43 | loop fusion | bytes 6291456 | tf_op jit(solution)/shard_map/slice | solution.py:70
  130.3 2.4 copy.62
  132.7 4.2 %copy.61 = f32[64,64,64]{0,1,2:T(8,128)} copy(f32[64,64,64]{2,1,0:T(8,128)} %get-tuple-element.177) | data formatting | bytes 2097152
  136.8 4.2 %copy.63 = f32[64,64,64]{0,1,2:T(8,128)} copy(f32[64,64,64]{2,1,0:T(8,128)} %get-tuple-element.178) | data formatting | bytes 2097152
  141.0 0.9 gather_fusion
  141.9 2.1 fusion.19
  144.0 0.1 copy-done
  144.1 2.4 maximum_bitcast_fusion
  146.5 6.4 %copy.53 = f32[64,1,129,64]{2,3,1,0:T(8,128)} copy(f32[64,1,129,64]{0,2,3,1:T(8,128)} %maximum_bitcast_fusion) | data formatting | bytes 4227072 | tf_op jit(solution)/shard_map/reshape | solution.py:16
  152.9 62.3 %all_to_all.5 = f32[64,1,129,64]{2,3,1,0:T(8,128)} all-to-all(f32[64,1,129,64]{2,3,1,0:T(8,128)} %copy.53), channel_id=1, replica_groups=mesh['sec_0'=4,'sec_1'=4,'sec_2'=4,'node'=2] {'sec_0','sec_1','sec_2'}, dimensions={0} | all-to-all | bytes 4227072 | tf_op jit(solution)/shard_map/all_to_all | solution.py:22
  215.2 2.5 reduce_sum.30
  217.7 0.1 slice_reduce_fusion
  217.8 0.1 copy.57
  217.9 0.1 fusion.21
  218.1 0.1 copy.55
  218.3 0.7 fusion.20
  219.0 7.3 %psum.28 = f32[]{:T(128)} all-reduce(f32[]{:T(128)} %fusion.20), channel_id=1, replica_groups=mesh['sec_0'=4,'sec_1'=4,'sec_2'=4,'node'=2] {'sec_0'}, use_global_device_ids=true, to_apply=%region_5.6 | all-reduce | flops 1 | bytes 8 | tf_op jit(solution)/shard_map/psum | solution.py:28
  226.3 10.5 %psum.29 = f32[]{:T(128)} all-reduce(f32[]{:T(128)} %psum.28), channel_id=1, replica_groups=mesh['sec_0'=4,'sec_1'=4,'sec_2'=4,'node'=2] {'sec_1'}, use_global_device_ids=true, to_apply=%region_6.7 | all-reduce | flops 1 | bytes 8 | tf_op jit(solution)/shard_map/psum | solution.py:28
  236.8 7.6 %psum.30 = f32[]{:T(128)} all-reduce(f32[]{:T(128)} %psum.29), channel_id=1, replica_groups=mesh['sec_0'=4,'sec_1'=4,'sec_2'=4,'node'=2] {'sec_2'}, use_global_device_ids=true, to_apply=%region_7.8 | all-reduce | flops 1 | bytes 8 | tf_op jit(solution)/shard_map/psum | solution.py:28
  244.4 0.1 maximum_bitcast_fusion.1
  244.5 9.3 %psum.31 = f32[]{:T(128)} all-reduce(f32[]{:T(128)} %psum.30), channel_id=1, replica_groups=mesh['sec_0'=4,'sec_1'=4,'sec_2'=4,'node'=2] {'node'}, use_global_device_ids=true, to_apply=%region_8.9 | all-reduce | flops 1 | bytes 8 | tf_op jit(solution)/shard_map/psum | solution.py:28
  254.5 0.6 maximum_multiply_fusion
  (21 shorter events, 1.0 us)
Async XLA Ops:
  141.9 2.2 copy-start
where the time goes:
time: 256 us; the launch traced here: 255 us
  matrix products  119 us (46%)
  blocking collectives  97 us (38%)
  local copies, waits for them, and re-layouts  27.1 us (11%)
  other arithmetic  10 us (4%)
    dot_general x12, matrix products, add_group(): lax.dot_general(selector, flat_terms, (((0,), (0,)), ((), ())), precision...  87.8 us
    all_to_all x1, blocking collectives, sum_at_owner(): lax.all_to_all(cut_along(shard, dim, length), axis, 0, 0, tiled=True)  62.3 us
    psum x4, blocking collectives, by_axis(): shard = lax.psum(shard, axis)  34.7 us
    dot_general x12, matrix products, add_group(): jnp.einsum('prc,prd->pcd', weights, product, preferred_element_type=jnp.f...  31.6 us
    unnamed x6, local copies, waits for them, and re-layouts  13.7 us
    reshape x1, local copies, waits for them, and re-layouts, cut_along(): shard.reshape(*shape[:dim], length, shape[dim] // length, *shape[dim + 1:])  6.38 us

commit v1 on v0

v1 whole, which is shorter than its diff:
```python
import functools

import jax
import jax.numpy as jnp
from jax import lax
from jax.experimental import pallas as pl
from jax.experimental.pallas import tpu as pltpu
from jax.sharding import Mesh
from jax.sharding import PartitionSpec as P

SEC = ("x", "y_hi", "y_lo", "z")
ALL = SEC + ("node",)
FAMILY = ("y_lo", "z", "node")
LOCAL = 8
DC = 128
HALF = 64
SLOTS = 384
CHUNK = 32
CHUNKS = SLOTS // CHUNK
PIECE = 40
F32 = jnp.float32


def rows_and_lanes(rows):
    row = lax.broadcasted_iota(jnp.int32, (rows, DC), 0)
    lane = lax.broadcasted_iota(jnp.int32, (rows, DC), 1)
    return row, lane


def partial_sums(live_ref, joined_ref, owner_ref, env, iso, out_ref, e_buf, w_buf, acc, e_sem, w_sem):
    live = live_ref[0, 0]
    chunks = (live + CHUNK - 1) // CHUNK

    def copies(chunk):
        here = pl.ds(chunk * CHUNK, CHUNK)
        return (
            pltpu.make_async_copy(env.at[0, here], e_buf.at[here], e_sem.at[chunk]),
            pltpu.make_async_copy(iso.at[0, here], w_buf.at[here], w_sem.at[chunk]),
        )

    def start(chunk, carry):
        for copy in copies(chunk):
            copy.start()
        return carry

    lax.fori_loop(0, chunks, start, 0)
    acc[...] = jnp.zeros_like(acc)

    def add_chunk(chunk, carry):
        for copy in copies(chunk):
            copy.wait()
        for u in range(CHUNK):
            slot = chunk * CHUNK + u
            weights = w_buf[slot]
            product = jnp.dot(e_buf[slot], weights, preferred_element_type=F32).astype(jnp.bfloat16)
            term = lax.dot_general(
                weights, product, (((0,), (0,)), ((), ())), preferred_element_type=F32
            )
            sector = jnp.where(slot < live, joined_ref[0, slot] & (LOCAL - 1), LOCAL)
            acc[sector] = acc[sector] + term
        return carry

    lax.fori_loop(0, chunks, add_chunk, 0)

    row, lane = rows_and_lanes(HALF)
    row8, lane8 = rows_and_lanes(8)
    family = 2 * lax.axis_index("x") + lax.axis_index("y_hi")
    packed, diagonals = [], []
    for j in range(LOCAL):
        top, bottom = acc[j, :HALF], acc[j, HALF:]
        turned = pltpu.roll(acc[j].T[HALF:], HALF, 1)
        packed.append(jnp.where(lane >= row, top, turned))
        diagonal = jnp.sum(jnp.where(lane == row + HALF, bottom, 0.0), axis=0, keepdims=True)
        owner = owner_ref[0, LOCAL * family + j].astype(F32)
        diagonals.append(jnp.where(lane8[:1] < HALF, owner, diagonal))
    diagonal_tile = jnp.concatenate(diagonals, axis=0)
    for v in range(8):
        rows = slice(8 * v, 8 * v + 8)
        for pair in range(LOCAL // 2):
            even, odd = packed[2 * pair][rows], packed[2 * pair + 1][rows]
            out_ref[2 * v, 8 * pair : 8 * pair + 8] = jnp.where(row8 < 4, even, odd)
            out_ref[2 * v + 1, 8 * pair : 8 * pair + 8] = jnp.where(row8 < 4, odd, even)
        out_ref[2 * v, 32:40] = diagonal_tile
        out_ref[2 * v + 1, 32:40] = diagonal_tile


def reduce_pieces(got_ref, out_ref):
    v = lax.axis_index("y_lo") * 4 + lax.axis_index("z")
    h = lax.axis_index("node")
    row, lane = rows_and_lanes(8)
    weight = jnp.where((lane < HALF) & (lane == row + 8 * v), 1.0, 2.0)
    first = HALF + 8 * v + 4 * h
    mine = (lane >= first) & (lane < first + 4)
    squares = jnp.zeros((8, DC), F32)
    summed = []
    for n in range(2):
        tiles = []
        for t in range(5):
            rows = slice(8 * t, 8 * t + 8)
            total = got_ref[n, rows]
            for source in range(1, 8):
                total = total + got_ref[2 * source + n, rows]
            tiles.append(total)
            squares = squares + jnp.where(mine, total * total, 0.0) if t == 4 else squares + weight * (total * total)
        summed.append(tiles)
    part = jnp.sum(squares)
    out_ref[...] = jnp.zeros_like(out_ref)
    out_ref[:, 0, 512:640] = jnp.full((128, DC), part, F32)
    for n in range(2):
        extra = summed[n][4]
        owners = (extra[:, :1] * 0.125).astype(jnp.int32)
        for j in range(LOCAL):
            slot = 2 * owners[j, 0] + n
            tile = summed[n][j // 2]
            low, high = tile[:4], tile[4:]
            mine4 = jnp.where(h == j % 2, low, high)
            for r in range(4):
                out_ref[slot, :, DC * r : DC * (r + 1)] = mine4[r : r + 1]
            out_ref[slot, :, 512:640] = jnp.where(lane[:1] < HALF, part, extra[j : j + 1])


def unpack(owner_ref, got_ref, out_ref, rows_buf):
    sec = (
        (lax.axis_index("x") * 2 + lax.axis_index("y_hi")) * 2 + lax.axis_index("y_lo")
    ) * 4 + lax.axis_index("z")
    sector = jnp.int32(0)
    for d in range(64):
        sector = jnp.where(owner_ref[0, d] == sec, d, sector)
    base = 16 * (sector // LOCAL)
    odd = sector % 2
    for v in range(8):
        for half in range(2):
            source = base + 2 * v + jnp.where(odd == 0, half, 1 - half)
            for r in range(4):
                rows_buf[8 * v + 4 * half + r : 8 * v + 4 * half + r + 1, :] = got_ref[
                    source, :, DC * r : DC * (r + 1)
                ]
    rows_buf[HALF:, :] = jnp.zeros((HALF, DC), F32)
    extra = got_ref[base, :, 512:640]
    total = jnp.sum(got_ref[:, 0, 512:640], axis=0, keepdims=True)[:, :1]
    factor = lax.rsqrt(total / (2 * 64 * DC * DC) + 1e-06)
    row, lane = rows_and_lanes(HALF)
    packed = rows_buf[:HALF, :]
    turned = rows_buf[...].T
    top = jnp.where(lane >= row, packed, turned[:HALF])
    inner = pltpu.roll(jnp.where(lane < row, packed, turned[:HALF]), HALF, 1)
    inner = jnp.where(lane == row + HALF, extra, inner)
    bottom = jnp.where(lane < HALF, turned[HALF:], inner)
    out_ref[0, 0, :HALF, :] = top * factor
    out_ref[0, 0, HALF:, :] = bottom * factor


def body(env_blocks, iso_blocks, joined_sector, owner_map, live_pairs):
    smem = pl.BlockSpec(memory_space=pltpu.SMEM)
    vmem = pl.BlockSpec(memory_space=pltpu.VMEM)
    hbm = pl.BlockSpec(memory_space=pl.ANY)
    pieces = pl.pallas_call(
        partial_sums,
        in_specs=[smem, smem, smem, hbm, hbm],
        out_specs=vmem,
        out_shape=jax.ShapeDtypeStruct((16, PIECE, DC), F32),
        scratch_shapes=[
            pltpu.VMEM((SLOTS, DC, DC), jnp.bfloat16),
            pltpu.VMEM((SLOTS, DC, DC), jnp.bfloat16),
            pltpu.VMEM((LOCAL + 1, DC, DC), F32),
            pltpu.SemaphoreType.DMA((CHUNKS,)),
            pltpu.SemaphoreType.DMA((CHUNKS,)),
        ],
        compiler_params=pltpu.CompilerParams(vmem_limit_bytes=48 << 20),
        name="partial_sums",
    )(live_pairs, joined_sector, owner_map, env_blocks, iso_blocks)
    pieces = lax.all_to_all(pieces, FAMILY, 0, 0, tiled=True)
    slots = pl.pallas_call(
        reduce_pieces,
        in_specs=[vmem],
        out_specs=vmem,
        out_shape=jax.ShapeDtypeStruct((128, 1, 640), F32),
        name="reduce_pieces",
    )(pieces)
    slots = lax.all_to_all(slots, ALL, 0, 0, tiled=True)
    return pl.pallas_call(
        unpack,
        in_specs=[smem, vmem],
        out_specs=vmem,
        out_shape=jax.ShapeDtypeStruct((1, 1, DC, DC), F32),
        scratch_shapes=[pltpu.VMEM((DC, DC), F32)],
        name="unpack",
    )(owner_map, slots)


def solution(mesh):
    split = Mesh(mesh.devices.reshape(4, 2, 2, 4, mesh.shape["node"]), ALL)
    placed = (
        P("node", SEC, None, None),
        P("node", SEC, None, None),
        P("node", SEC),
        P("node", None),
        P("node", SEC),
    )
    return jax.shard_map(
        body, mesh=split, in_specs=placed, out_specs=P("node", SEC, None, None), check_vma=False
    )
```

time: 256 us -> 51.3 us (0.20)
  matrix products: 119 us -> 0 us
  blocking collectives: 97 us -> 37.1 us
  local copies, waits for them, and re-layouts: 27.1 us -> 1.33 us
  Pallas kernels: 0 us -> 11.3 us
  other arithmetic: 10 us -> 0 us
    dot_general x24 -> x0, matrix products: 119 us -> none  [the longest x12 87.8 us: add_group(): lax.dot_general(selector, flat_terms, (((0,), (0,)), ((), ())), precision...]
    psum x4 -> x0, blocking collectives: 34.7 us -> none  [by_axis(): shard = lax.psum(shard, axis)]
    all_to_all x1 -> x2, blocking collectives: 62.3 us -> 37.1 us  [the longest x1 18.8 us: body(): pieces = lax.all_to_all(pieces, FAMILY, 0, 0, tiled=True)]
    unnamed x6 -> x4, local copies, waits for them, and re-layouts: 13.7 us -> 1.33 us
    pallas_call x0 -> x3, Pallas kernels: none -> 11.3 us  [the longest x1 7.54 us: body(): pl.pallas_call(partial_sums, in_specs=[smem, smem, smem, hbm, hbm], out_s...]
    reshape x1 -> x0, local copies, waits for them, and re-layouts: 6.38 us -> none  [cut_along(): shard.reshape(*shape[:dim], length, shape[dim] // length, *shape[dim + 1:])]
    slice x4 -> x0, local copies, waits for them, and re-layouts: 4.06 us -> none  [the longest x1 3.8 us: body(): upper_left = partial_value[:, :half_width, :half_width]]
    reduce_sum x3 -> x0, other arithmetic: 3.93 us -> none  [the longest x1 2.48 us: sum_at_owner(): return jnp.sum(blocks, axis=0)]
where the time goes in v1:
time: 51.3 us; the launch traced here: 50.3 us
  blocking collectives  37.1 us (72%)
  Pallas kernels  11.3 us (22%)
  local copies, waits for them, and re-layouts  1.33 us (3%)
  between operations  0.67 us (1%)
    all_to_all x1, blocking collectives, body(): pieces = lax.all_to_all(pieces, FAMILY, 0, 0, tiled=True)  18.8 us
    all_to_all x1, blocking collectives, body(): slots = lax.all_to_all(slots, ALL, 0, 0, tiled=True)  18.3 us
    pallas_call x1, Pallas kernels, body(): pl.pallas_call(partial_sums, in_specs=[smem, smem, smem, hbm, hbm], out_s...  7.54 us
    pallas_call x1, Pallas kernels, body(): pl.pallas_call(reduce_pieces, in_specs=[vmem], out_specs=vmem, out_shape=...  1.89 us
    pallas_call x1, Pallas kernels, body(): pl.pallas_call(unpack, in_specs=[smem, vmem], out_specs=vmem, out_shape=j...  1.85 us
    unnamed x4, local copies, waits for them, and re-layouts  1.33 us

profile of v1, /device:TPU:1, one launch (start us, length us, event | category | flops | bytes accessed | tf_op | source)
XLA Modules:
  0.0 50.3 jit_solution(16701403283726734834)
XLA Ops:
  0.7 0.0 copy-start
  0.7 0.6 %copy-done = s32[1,64]{1,0:T(1,128)S(1)} copy-done((s32[1,64]{1,0:T(1,128)S(1)}, s32[1,64]{1,0:T(1,128)}, u32[]{:S(2)}) %copy-start) | copy-done | bytes 280
  1.3 0.0 copy-start.1
  1.3 0.7 %copy-done.1 = s32[1,384]{1,0:T(1,128)S(1)} copy-done((s32[1,384]{1,0:T(1,128)S(1)}, s32[1,384]{1,0:T(1,128)}, u32[]{:S(2)}) %copy-start.1) | copy-done | bytes 1560
  2.0 7.5 %partial_sums.1 = f32[16,40,128]{2,1,0:T(8,128)S(1)} custom-call(s32[1,1]{1,0:T(1,128)S(6)} %copy.6.live_ref, s32[1,384]{1,0:T(1,128)S(1)} %copy-done.1, s32[1,64]{1,0:T(1,128)S(1)} %copy-done, bf16[1,384,128,128]{3,2,1,0:T(8,128)(2,1)} %env.1, bf16[1,384,128,128]{3,2,1,0:T(8,128)(2,1)} %iso.1), custom_call_target="tpu_custom_call" | custom-call | tf_op jit(solution)/shard_map/partial_sums/pallas_call | solution.py:157
  9.5 18.8 %all_to_all.10.got_ref = f32[16,40,128]{2,1,0:T(8,128)} all-to-all(f32[16,40,128]{2,1,0:T(8,128)S(1)} %partial_sums.1), channel_id=1, replica_groups=mesh['x'=4,'y_hi'=2,'y_lo'=2,'z'=4,'node'=2] {'y_lo','z','node'}, dimensions={0} | all-to-all | bytes 655360 | tf_op jit(solution)/shard_map/all_to_all | solution.py:172
  28.3 1.9 %reduce_pieces.1 = f32[128,1,640]{2,1,0:T(1,128)} custom-call(f32[16,40,128]{2,1,0:T(8,128)} %all_to_all.10.got_ref), custom_call_target="tpu_custom_call" | custom-call | tf_op jit(solution)/shard_map/reduce_pieces/pallas_call | solution.py:173
  30.2 18.3 %all_to_all.11.got_ref = f32[128,1,640]{2,1,0:T(1,128)} all-to-all(f32[128,1,640]{2,1,0:T(1,128)} %reduce_pieces.1), channel_id=1, replica_groups=mesh['x'=4,'y_hi'=2,'y_lo'=2,'z'=4,'node'=2] {'x','y_hi','y_lo','z','node'}, dimensions={0} | all-to-all | bytes 655360 | tf_op jit(solution)/shard_map/all_to_all | solution.py:180
  48.5 1.8 %unpack.1 = f32[1,1,128,128]{3,2,1,0:T(8,128)} custom-call(s32[1,64]{1,0:T(1,128)} %owner_ref.3, f32[128,1,640]{2,1,0:T(1,128)} %all_to_all.11.got_ref), custom_call_target="tpu_custom_call" | custom-call | tf_op jit(solution)/shard_map/unpack/pallas_call | solution.py:181
Async XLA Ops:
  0.7 0.7 %copy-start = (s32[1,64]{1,0:T(1,128)S(1)}, s32[1,64]{1,0:T(1,128)}, u32[]{:S(2)}) copy-start(s32[1,64]{1,0:T(1,128)} %owner_ref.3) | copy-start | bytes 772
  1.3 0.7 %copy-start.1 = (s32[1,384]{1,0:T(1,128)S(1)}, s32[1,384]{1,0:T(1,128)}, u32[]{:S(2)}) copy-start(s32[1,384]{1,0:T(1,128)} %joined_ref.1) | copy-start | bytes 4612

commit v2 on v1

--- a/solution.py
+++ b/solution.py
@@ -15,7 +15,7 @@
 DC = 128
 HALF = 64
 SLOTS = 384
-CHUNK = 32
+CHUNK = 64
 CHUNKS = SLOTS // CHUNK
 PIECE = 40
 F32 = jnp.float32
@@ -27,9 +27,18 @@
     return row, lane
 
 
-def partial_sums(live_ref, joined_ref, owner_ref, env, iso, out_ref, e_buf, w_buf, acc, e_sem, w_sem):
-    live = live_ref[0, 0]
-    chunks = (live + CHUNK - 1) // CHUNK
+def partial_sums(
+    live_hbm, joined_hbm, owner_hbm, env, iso, out_ref, sector_ref,
+    e_buf, w_buf, acc, live_ref, joined_ref, owner_ref, e_sem, w_sem, small_sem,
+):
+    small = [
+        pltpu.make_async_copy(source, target, small_sem.at[i])
+        for i, (source, target) in enumerate(
+            ((live_hbm, live_ref), (joined_hbm, joined_ref), (owner_hbm, owner_ref))
+        )
+    ]
+    for copy in small:
+        copy.start()
 
     def copies(chunk):
         here = pl.ds(chunk * CHUNK, CHUNK)
@@ -43,8 +52,20 @@
             copy.start()
         return carry
 
-    lax.fori_loop(0, chunks, start, 0)
+    start(0, 0)
     acc[...] = jnp.zeros_like(acc)
+    small[0].wait()
+    live = live_ref[0, 0]
+    chunks = (live + CHUNK - 1) // CHUNK
+    lax.fori_loop(1, chunks, start, 0)
+    small[1].wait()
+    small[2].wait()
+    sec = (
+        (lax.axis_index("x") * 2 + lax.axis_index("y_hi")) * 2 + lax.axis_index("y_lo")
+    ) * 4 + lax.axis_index("z")
+    sector_ref[0, 0] = lax.fori_loop(
+        0, 64, lambda d, found: jnp.where(owner_ref[0, d] == sec, d, found), jnp.int32(0)
+    )
 
     def add_chunk(chunk, carry):
         for copy in copies(chunk):
@@ -119,13 +140,8 @@
             out_ref[slot, :, 512:640] = jnp.where(lane[:1] < HALF, part, extra[j : j + 1])
 
 
-def unpack(owner_ref, got_ref, out_ref, rows_buf):
-    sec = (
-        (lax.axis_index("x") * 2 + lax.axis_index("y_hi")) * 2 + lax.axis_index("y_lo")
-    ) * 4 + lax.axis_index("z")
-    sector = jnp.int32(0)
-    for d in range(64):
-        sector = jnp.where(owner_ref[0, d] == sec, d, sector)
+def unpack(sector_ref, got_ref, out_ref, rows_buf):
+    sector = sector_ref[0, 0]
     base = 16 * (sector // LOCAL)
     odd = sector % 2
     for v in range(8):
@@ -153,18 +169,25 @@
 def body(env_blocks, iso_blocks, joined_sector, owner_map, live_pairs):
     smem = pl.BlockSpec(memory_space=pltpu.SMEM)
     vmem = pl.BlockSpec(memory_space=pltpu.VMEM)
-    hbm = pl.BlockSpec(memory_space=pl.ANY)
-    pieces = pl.pallas_call(
+    hbm = pl.BlockSpec(memory_space=pltpu.HBM)
+    pieces, sector = pl.pallas_call(
         partial_sums,
-        in_specs=[smem, smem, smem, hbm, hbm],
-        out_specs=vmem,
-        out_shape=jax.ShapeDtypeStruct((16, PIECE, DC), F32),
+        in_specs=[hbm] * 5,
+        out_specs=[vmem, smem],
+        out_shape=[
+            jax.ShapeDtypeStruct((16, PIECE, DC), F32),
+            jax.ShapeDtypeStruct((1, 1), jnp.int32),
+        ],
         scratch_shapes=[
             pltpu.VMEM((SLOTS, DC, DC), jnp.bfloat16),
             pltpu.VMEM((SLOTS, DC, DC), jnp.bfloat16),
             pltpu.VMEM((LOCAL + 1, DC, DC), F32),
+            pltpu.SMEM((1, 1), jnp.int32),
+            pltpu.SMEM((1, SLOTS), jnp.int32),
+            pltpu.SMEM((1, 64), jnp.int32),
             pltpu.SemaphoreType.DMA((CHUNKS,)),
             pltpu.SemaphoreType.DMA((CHUNKS,)),
+            pltpu.SemaphoreType.DMA((3,)),
         ],
         compiler_params=pltpu.CompilerParams(vmem_limit_bytes=48 << 20),
         name="partial_sums",
@@ -175,6 +198,7 @@
         in_specs=[vmem],
         out_specs=vmem,
         out_shape=jax.ShapeDtypeStruct((128, 1, 640), F32),
+        compiler_params=pltpu.CompilerParams(vmem_limit_bytes=8 << 20),
         name="reduce_pieces",
     )(pieces)
     slots = lax.all_to_all(slots, ALL, 0, 0, tiled=True)
@@ -184,8 +208,9 @@
         out_specs=vmem,
         out_shape=jax.ShapeDtypeStruct((1, 1, DC, DC), F32),
         scratch_shapes=[pltpu.VMEM((DC, DC), F32)],
+        compiler_params=pltpu.CompilerParams(vmem_limit_bytes=8 << 20),
         name="unpack",
-    )(owner_map, slots)
+    )(sector, slots)
 
 
 def solution(mesh):

time: 51.3 us -> 48 us (0.936); the launches traced: 50.3 us -> 48.6 us
  Pallas kernels: 11.3 us -> 10 us
    all_to_all x1, blocking collectives: 18.8 us -> 16.5 us  [body(): pieces = lax.all_to_all(pieces, FAMILY, 0, 0, tiled=True)]
    all_to_all x1, blocking collectives: 18.3 us -> 20.1 us  [body(): slots = lax.all_to_all(slots, ALL, 0, 0, tiled=True)]
    pallas_call x1, Pallas kernels: 1.89 us -> 0.22 us  [body(): pl.pallas_call(reduce_pieces, in_specs=[vmem], out_specs=vmem, out_shape=...]
    pallas_call x1, Pallas kernels: 7.54 us -> 8.37 us  [body(): pl.pallas_call(partial_sums, in_specs=[hbm] * 5, out_specs=[vmem, smem],...]
where the time goes in v2:
time: 48 us; the launch traced here: 48.6 us
  blocking collectives  36.6 us (76%)
  Pallas kernels  10 us (21%)
  local copies, waits for them, and re-layouts  1.33 us (3%)
  between operations  0.68 us (1%)
    all_to_all x1, blocking collectives, body(): slots = lax.all_to_all(slots, ALL, 0, 0, tiled=True)  20.1 us
    all_to_all x1, blocking collectives, body(): pieces = lax.all_to_all(pieces, FAMILY, 0, 0, tiled=True)  16.5 us
    pallas_call x1, Pallas kernels, body(): pl.pallas_call(partial_sums, in_specs=[hbm] * 5, out_specs=[vmem, smem],...  8.37 us
    pallas_call x1, Pallas kernels, body(): pl.pallas_call(unpack, in_specs=[smem, vmem], out_specs=vmem, out_shape=j...  1.44 us
    unnamed x4, local copies, waits for them, and re-layouts  1.33 us

profile of v2, /device:TPU:1, one launch (start us, length us, event | category | flops | bytes accessed | tf_op | source)
XLA Modules:
  0.0 48.6 jit_solution(14186236528394656885)
XLA Ops:
  0.7 0.0 copy-start
  0.7 0.7 %copy-done = s32[1,384]{1,0:T(1,128)S(1)} copy-done((s32[1,384]{1,0:T(1,128)S(1)}, s32[1,384]{1,0:T(1,128)}, u32[]{:S(2)}) %copy-start) | copy-done | bytes 1560
  1.3 0.0 copy-start.1
  1.3 0.7 %copy-done.1 = s32[1,64]{1,0:T(1,128)S(1)} copy-done((s32[1,64]{1,0:T(1,128)S(1)}, s32[1,64]{1,0:T(1,128)}, u32[]{:S(2)}) %copy-start.1) | copy-done | bytes 280
  2.0 8.4 %partial_sums.1 = (f32[16,40,128]{2,1,0:T(8,128)S(1)}, s32[1,1]{1,0:T(1,128)}) custom-call(s32[1,1]{1,0:T(1,128)S(6)} %copy.6.live_hbm, s32[1,384]{1,0:T(1,128)S(1)} %copy-done, s32[1,64]{1,0:T(1,128)S(1)} %copy-done.1, bf16[1,384,128,128]{3,2,1,0:T(8,128)(2,1)} %env.1, bf16[1,384,128,128]{3,2,1,0:T(8,128)(2,1)} %iso.1), custom_call_target="tpu_custom_call" | custom-call | tf_op jit(solution)/shard_map/partial_sums/pallas_call | solution.py:173
  10.4 16.5 %all_to_all.10.got_ref = f32[16,40,128]{2,1,0:T(8,128)S(1)} all-to-all(f32[16,40,128]{2,1,0:T(8,128)S(1)} %get-tuple-element.8), channel_id=1, replica_groups=mesh['x'=4,'y_hi'=2,'y_lo'=2,'z'=4,'node'=2] {'y_lo','z','node'}, dimensions={0} | all-to-all | bytes 655360 | tf_op jit(solution)/shard_map/all_to_all | solution.py:195
  26.9 0.2 reduce_pieces.1
  27.1 20.1 %all_to_all.11.got_ref = f32[128,1,640]{2,1,0:T(1,128)S(1)} all-to-all(f32[128,1,640]{2,1,0:T(1,128)S(1)} %reduce_pieces.1), channel_id=1, replica_groups=mesh['x'=4,'y_hi'=2,'y_lo'=2,'z'=4,'node'=2] {'x','y_hi','y_lo','z','node'}, dimensions={0} | all-to-all | bytes 655360 | tf_op jit(solution)/shard_map/all_to_all | solution.py:204
  47.2 1.4 %unpack.1 = f32[1,1,128,128]{3,2,1,0:T(8,128)} custom-call(s32[1,1]{1,0:T(1,128)} %get-tuple-element.7.sector_ref, f32[128,1,640]{2,1,0:T(1,128)S(1)} %all_to_all.11.got_ref), custom_call_target="tpu_custom_call" | custom-call | tf_op jit(solution)/shard_map/unpack/pallas_call | solution.py:205
Async XLA Ops:
  0.7 0.7 %copy-start = (s32[1,384]{1,0:T(1,128)S(1)}, s32[1,384]{1,0:T(1,128)}, u32[]{:S(2)}) copy-start(s32[1,384]{1,0:T(1,128)} %joined_hbm.1) | copy-start | bytes 4612
  1.3 0.7 %copy-start.1 = (s32[1,64]{1,0:T(1,128)S(1)}, s32[1,64]{1,0:T(1,128)}, u32[]{:S(2)}) copy-start(s32[1,64]{1,0:T(1,128)} %owner_hbm.1) | copy-start | bytes 772

commit v3 on v2

--- a/solution.py
+++ b/solution.py
@@ -28,13 +28,13 @@
 
 
 def partial_sums(
-    live_hbm, joined_hbm, owner_hbm, env, iso, out_ref, sector_ref,
-    e_buf, w_buf, acc, live_ref, joined_ref, owner_ref, e_sem, w_sem, small_sem,
+    live_ref, joined_hbm, owner_hbm, env, iso, out_ref, sector_ref,
+    e_buf, w_buf, acc, joined_ref, owner_ref, e_sem, w_sem, small_sem,
 ):
     small = [
         pltpu.make_async_copy(source, target, small_sem.at[i])
         for i, (source, target) in enumerate(
-            ((live_hbm, live_ref), (joined_hbm, joined_ref), (owner_hbm, owner_ref))
+            ((joined_hbm, joined_ref), (owner_hbm, owner_ref))
         )
     ]
     for copy in small:
@@ -52,20 +52,19 @@
             copy.start()
         return carry
 
-    start(0, 0)
-    acc[...] = jnp.zeros_like(acc)
-    small[0].wait()
     live = live_ref[0, 0]
     chunks = (live + CHUNK - 1) // CHUNK
-    lax.fori_loop(1, chunks, start, 0)
-    small[1].wait()
-    small[2].wait()
+    lax.fori_loop(0, chunks, start, 0)
+    acc[...] = jnp.zeros_like(acc)
+    for copy in small:
+        copy.wait()
     sec = (
         (lax.axis_index("x") * 2 + lax.axis_index("y_hi")) * 2 + lax.axis_index("y_lo")
     ) * 4 + lax.axis_index("z")
-    sector_ref[0, 0] = lax.fori_loop(
+    sector = lax.fori_loop(
         0, 64, lambda d, found: jnp.where(owner_ref[0, d] == sec, d, found), jnp.int32(0)
     )
+    sector_ref[...] = jnp.full((8, DC), sector, jnp.int32)
 
     def add_chunk(chunk, carry):
         for copy in copies(chunk):
@@ -141,7 +140,7 @@
 
 
 def unpack(sector_ref, got_ref, out_ref, rows_buf):
-    sector = sector_ref[0, 0]
+    sector = sector_ref[:1, :1][0, 0]
     base = 16 * (sector // LOCAL)
     odd = sector % 2
     for v in range(8):
@@ -172,26 +171,31 @@
     hbm = pl.BlockSpec(memory_space=pltpu.HBM)
     pieces, sector = pl.pallas_call(
         partial_sums,
-        in_specs=[hbm] * 5,
-        out_specs=[vmem, smem],
+        in_specs=[smem] + [hbm] * 4,
+        out_specs=[vmem, vmem],
         out_shape=[
             jax.ShapeDtypeStruct((16, PIECE, DC), F32),
-            jax.ShapeDtypeStruct((1, 1), jnp.int32),
+            jax.ShapeDtypeStruct((8, DC), jnp.int32),
         ],
         scratch_shapes=[
             pltpu.VMEM((SLOTS, DC, DC), jnp.bfloat16),
             pltpu.VMEM((SLOTS, DC, DC), jnp.bfloat16),
             pltpu.VMEM((LOCAL + 1, DC, DC), F32),
-            pltpu.SMEM((1, 1), jnp.int32),
             pltpu.SMEM((1, SLOTS), jnp.int32),
             pltpu.SMEM((1, 64), jnp.int32),
             pltpu.SemaphoreType.DMA((CHUNKS,)),
             pltpu.SemaphoreType.DMA((CHUNKS,)),
-            pltpu.SemaphoreType.DMA((3,)),
+            pltpu.SemaphoreType.DMA((2,)),
         ],
         compiler_params=pltpu.CompilerParams(vmem_limit_bytes=48 << 20),
         name="partial_sums",
-    )(live_pairs, joined_sector, owner_map, env_blocks, iso_blocks)
+    )(
+        live_pairs,
+        pltpu.with_memory_space_constraint(joined_sector, pltpu.HBM),
+        pltpu.with_memory_space_constraint(owner_map, pltpu.HBM),
+        env_blocks,
+        iso_blocks,
+    )
     pieces = lax.all_to_all(pieces, FAMILY, 0, 0, tiled=True)
     slots = pl.pallas_call(
         reduce_pieces,
@@ -204,7 +208,7 @@
     slots = lax.all_to_all(slots, ALL, 0, 0, tiled=True)
     return pl.pallas_call(
         unpack,
-        in_specs=[smem, vmem],
+        in_specs=[vmem, vmem],
         out_specs=vmem,
         out_shape=jax.ShapeDtypeStruct((1, 1, DC, DC), F32),
         scratch_shapes=[pltpu.VMEM((DC, DC), F32)],

time: 48 us -> 45.6 us (0.950); the launches traced: 48.6 us -> 44.8 us
  Pallas kernels: 10 us -> 5.08 us
  blocking collectives: 36.6 us -> 39 us
  local copies, waits for them, and re-layouts: 1.33 us -> 0 us
    pallas_call x2, Pallas kernels: 9.81 us -> 4.86 us  [the longest x1 4.02 us: body(): pl.pallas_call(partial_sums, in_specs=[smem] + [hbm] * 4, out_specs=[vmem...]
    all_to_all x1, blocking collectives: 16.5 us -> 20.8 us  [body(): pieces = lax.all_to_all(pieces, FAMILY, 0, 0, tiled=True)]
    all_to_all x1, blocking collectives: 20.1 us -> 18.3 us  [body(): slots = lax.all_to_all(slots, ALL, 0, 0, tiled=True)]
    unnamed x4 -> x0, local copies, waits for them, and re-layouts: 1.33 us -> none
where the time goes in v3:
time: 45.6 us; the launch traced here: 44.8 us
  blocking collectives  39 us (86%)
  Pallas kernels  5.08 us (11%)
  between operations  0.67 us (1%)
    all_to_all x1, blocking collectives, body(): pieces = lax.all_to_all(pieces, FAMILY, 0, 0, tiled=True)  20.8 us
    all_to_all x1, blocking collectives, body(): slots = lax.all_to_all(slots, ALL, 0, 0, tiled=True)  18.3 us
    pallas_call x1, Pallas kernels, body(): pl.pallas_call(partial_sums, in_specs=[smem] + [hbm] * 4, out_specs=[vmem...  4.02 us

profile of v3, /device:TPU:1, one launch (start us, length us, event | category | flops | bytes accessed | tf_op | source)
XLA Modules:
  0.0 44.8 jit_solution(12339483395019586968)
XLA Ops:
  0.7 4.0 %partial_sums.1 = (f32[16,40,128]{2,1,0:T(8,128)S(1)}, s32[8,128]{1,0:T(8,128)S(1)}) custom-call(s32[1,1]{1,0:T(1,128)S(6)} %copy.6.live_ref, s32[1,384]{1,0:T(1,128)} %joined_hbm.1, s32[1,64]{1,0:T(1,128)} %owner_hbm.1, bf16[1,384,128,128]{3,2,1,0:T(8,128)(2,1)} %env.1, bf16[1,384,128,128]{3,2,1,0:T(8,128)(2,1)} %iso.1), custom_call_target="tpu_custom_call" | custom-call | tf_op jit(solution)/shard_map/partial_sums/pallas_call | solution.py:172
  4.7 20.8 %all_to_all.10.got_ref = f32[16,40,128]{2,1,0:T(8,128)S(1)} all-to-all(f32[16,40,128]{2,1,0:T(8,128)S(1)} %get-tuple-element.8), channel_id=1, replica_groups=mesh['x'=4,'y_hi'=2,'y_lo'=2,'z'=4,'node'=2] {'y_lo','z','node'}, dimensions={0} | all-to-all | bytes 655360 | tf_op jit(solution)/shard_map/all_to_all | solution.py:199
  25.5 0.2 reduce_pieces.1
  25.7 18.3 %all_to_all.11.got_ref = f32[128,1,640]{2,1,0:T(1,128)S(1)} all-to-all(f32[128,1,640]{2,1,0:T(1,128)S(1)} %reduce_pieces.1), channel_id=1, replica_groups=mesh['x'=4,'y_hi'=2,'y_lo'=2,'z'=4,'node'=2] {'x','y_hi','y_lo','z','node'}, dimensions={0} | all-to-all | bytes 655360 | tf_op jit(solution)/shard_map/all_to_all | solution.py:208
  44.0 0.8 %unpack.1 = f32[1,1,128,128]{3,2,1,0:T(8,128)} custom-call(s32[8,128]{1,0:T(8,128)S(1)} %get-tuple-element.7.sector_ref, f32[128,1,640]{2,1,0:T(1,128)S(1)} %all_to_all.11.got_ref), custom_call_target="tpu_custom_call" | custom-call | tf_op jit(solution)/shard_map/unpack/pallas_call | solution.py:209

commit v4 on v3

--- a/solution.py
+++ b/solution.py
@@ -88,7 +88,8 @@
     packed, diagonals = [], []
     for j in range(LOCAL):
         top, bottom = acc[j, :HALF], acc[j, HALF:]
-        turned = pltpu.roll(acc[j].T[HALF:], HALF, 1)
+        turned = bottom.T[HALF:]
+        turned = jnp.concatenate([turned, jnp.zeros_like(turned)], axis=1)
         packed.append(jnp.where(lane >= row, top, turned))
         diagonal = jnp.sum(jnp.where(lane == row + HALF, bottom, 0.0), axis=0, keepdims=True)
         owner = owner_ref[0, LOCAL * family + j].astype(F32)

time: 45.6 us -> 45.6 us (level)
  Pallas kernels: 5.08 us -> 9.11 us
  blocking collectives: 39 us -> 35.2 us
    all_to_all x1, blocking collectives: 20.8 us -> 15.9 us  [body(): pieces = lax.all_to_all(pieces, FAMILY, 0, 0, tiled=True)]
    pallas_call x1, Pallas kernels: 4.02 us -> 8.04 us  [body(): pl.pallas_call(partial_sums, in_specs=[smem] + [hbm] * 4, out_specs=[vmem...]
    all_to_all x1, blocking collectives: 18.3 us -> 19.3 us  [body(): slots = lax.all_to_all(slots, ALL, 0, 0, tiled=True)]
where the time goes in v4:
time: 45.6 us; the launch traced here: 45 us
  blocking collectives  35.2 us (77%)
  Pallas kernels  9.11 us (20%)
  between operations  0.67 us (1%)
    all_to_all x1, blocking collectives, body(): slots = lax.all_to_all(slots, ALL, 0, 0, tiled=True)  19.3 us
    all_to_all x1, blocking collectives, body(): pieces = lax.all_to_all(pieces, FAMILY, 0, 0, tiled=True)  15.9 us
    pallas_call x1, Pallas kernels, body(): pl.pallas_call(partial_sums, in_specs=[smem] + [hbm] * 4, out_specs=[vmem...  8.04 us

profile of v4, /device:TPU:1, one launch (start us, length us, event | category | flops | bytes accessed | tf_op | source)
XLA Modules:
  0.0 45.0 jit_solution(6606900094535502141)
XLA Ops:
  0.7 8.0 %partial_sums.1 = (f32[16,40,128]{2,1,0:T(8,128)S(1)}, s32[8,128]{1,0:T(8,128)S(1)}) custom-call(s32[1,1]{1,0:T(1,128)S(6)} %copy.6.live_ref, s32[1,384]{1,0:T(1,128)} %joined_hbm.1, s32[1,64]{1,0:T(1,128)} %owner_hbm.1, bf16[1,384,128,128]{3,2,1,0:T(8,128)(2,1)} %env.1, bf16[1,384,128,128]{3,2,1,0:T(8,128)(2,1)} %iso.1), custom_call_target="tpu_custom_call" | custom-call | tf_op jit(solution)/shard_map/partial_sums/pallas_call | solution.py:173
  8.7 15.9 %all_to_all.10.got_ref = f32[16,40,128]{2,1,0:T(8,128)S(1)} all-to-all(f32[16,40,128]{2,1,0:T(8,128)S(1)} %get-tuple-element.8), channel_id=1, replica_groups=mesh['x'=4,'y_hi'=2,'y_lo'=2,'z'=4,'node'=2] {'y_lo','z','node'}, dimensions={0} | all-to-all | bytes 655360 | tf_op jit(solution)/shard_map/all_to_all | solution.py:200
  24.6 0.2 reduce_pieces.1
  24.9 19.3 %all_to_all.11.got_ref = f32[128,1,640]{2,1,0:T(1,128)S(1)} all-to-all(f32[128,1,640]{2,1,0:T(1,128)S(1)} %reduce_pieces.1), channel_id=1, replica_groups=mesh['x'=4,'y_hi'=2,'y_lo'=2,'z'=4,'node'=2] {'x','y_hi','y_lo','z','node'}, dimensions={0} | all-to-all | bytes 655360 | tf_op jit(solution)/shard_map/all_to_all | solution.py:209
  44.1 0.8 %unpack.1 = f32[1,1,128,128]{3,2,1,0:T(8,128)} custom-call(s32[8,128]{1,0:T(8,128)S(1)} %get-tuple-element.7.sector_ref, f32[128,1,640]{2,1,0:T(1,128)S(1)} %all_to_all.11.got_ref), custom_call_target="tpu_custom_call" | custom-call | tf_op jit(solution)/shard_map/unpack/pallas_call | solution.py:210

commit v5 on v4

--- a/solution.py
+++ b/solution.py
@@ -48,8 +48,8 @@
         )
 
     def start(chunk, carry):
-        for copy in copies(chunk):
-            copy.start()
+        for queue, copy in enumerate(copies(chunk)):
+            copy.start(priority=queue)
         return carry
 
     live = live_ref[0, 0]

time: 45.6 us -> 48 us (1.053); the launches traced: 45 us -> 48.5 us
  blocking collectives: 35.2 us -> 38.9 us
    all_to_all x1, blocking collectives: 15.9 us -> 19.1 us  [body(): pieces = lax.all_to_all(pieces, FAMILY, 0, 0, tiled=True)]
    all_to_all x1, blocking collectives: 19.3 us -> 19.8 us  [body(): slots = lax.all_to_all(slots, ALL, 0, 0, tiled=True)]
where the time goes in v5:
time: 48 us; the launch traced here: 48.5 us
  blocking collectives  38.9 us (81%)
  Pallas kernels  8.97 us (19%)
  between operations  0.67 us (1%)
    all_to_all x1, blocking collectives, body(): slots = lax.all_to_all(slots, ALL, 0, 0, tiled=True)  19.8 us
    all_to_all x1, blocking collectives, body(): pieces = lax.all_to_all(pieces, FAMILY, 0, 0, tiled=True)  19.1 us
    pallas_call x1, Pallas kernels, body(): pl.pallas_call(partial_sums, in_specs=[smem] + [hbm] * 4, out_specs=[vmem...  7.91 us

profile of v5, /device:TPU:1, one launch (start us, length us, event | category | flops | bytes accessed | tf_op | source)
XLA Modules:
  0.0 48.5 jit_solution(17771337693387186405)
XLA Ops:
  0.7 7.9 %partial_sums.1 = (f32[16,40,128]{2,1,0:T(8,128)S(1)}, s32[8,128]{1,0:T(8,128)S(1)}) custom-call(s32[1,1]{1,0:T(1,128)S(6)} %copy.6.live_ref, s32[1,384]{1,0:T(1,128)} %joined_hbm.1, s32[1,64]{1,0:T(1,128)} %owner_hbm.1, bf16[1,384,128,128]{3,2,1,0:T(8,128)(2,1)} %env.1, bf16[1,384,128,128]{3,2,1,0:T(8,128)(2,1)} %iso.1), custom_call_target="tpu_custom_call" | custom-call | tf_op jit(solution)/shard_map/partial_sums/pallas_call | solution.py:173
  8.6 19.1 %all_to_all.10.got_ref = f32[16,40,128]{2,1,0:T(8,128)S(1)} all-to-all(f32[16,40,128]{2,1,0:T(8,128)S(1)} %get-tuple-element.8), channel_id=1, replica_groups=mesh['x'=4,'y_hi'=2,'y_lo'=2,'z'=4,'node'=2] {'y_lo','z','node'}, dimensions={0} | all-to-all | bytes 655360 | tf_op jit(solution)/shard_map/all_to_all | solution.py:200
  27.6 0.2 reduce_pieces.1
  27.9 19.8 %all_to_all.11.got_ref = f32[128,1,640]{2,1,0:T(1,128)S(1)} all-to-all(f32[128,1,640]{2,1,0:T(1,128)S(1)} %reduce_pieces.1), channel_id=1, replica_groups=mesh['x'=4,'y_hi'=2,'y_lo'=2,'z'=4,'node'=2] {'x','y_hi','y_lo','z','node'}, dimensions={0} | all-to-all | bytes 655360 | tf_op jit(solution)/shard_map/all_to_all | solution.py:209
  47.7 0.8 %unpack.1 = f32[1,1,128,128]{3,2,1,0:T(8,128)} custom-call(s32[8,128]{1,0:T(8,128)S(1)} %get-tuple-element.7.sector_ref, f32[128,1,640]{2,1,0:T(1,128)S(1)} %all_to_all.11.got_ref), custom_call_target="tpu_custom_call" | custom-call | tf_op jit(solution)/shard_map/unpack/pallas_call | solution.py:210
